TPU v7x, 32 devices: a whole 2x2x4 slice. The times are simulated.
32 devices in a mesh: gx: 4 (over y, core), gy: 4 (over z), gz: 2 (over x).
Axes of the slice: x: 2, y: 2, z: 4, core: 2. Of those that a mesh axis runs over, the one named last changes fastest.
Arguments:
- rhs: float32 [4, 32, 32, 256], P(None, 'gx', 'gy', 'gz'), may hold values from -170 to 170
- basis: bfloat16 [4, 8, 32, 32, 256], P(None, None, 'gx', 'gy', 'gz'), may hold values from -6 to 6
- inertia: float32 [32, 32, 256], P('gx', 'gy', 'gz'), may hold values from 0.5 to 2
- helm: float32 [4], replicated, may hold values from 0.2 to 1
- stiffness: float32 [8, 8], replicated, may hold values from -0.05 to 0.6, as said below
Outputs:
- solution: float32 [4, 32, 32, 256], P(None, 'gx', 'gy', 'gz')
- new_basis: bfloat16 [4, 32, 32, 256], P(None, 'gx', 'gy', 'gz')
Inputs may be any that keep to these rules, and one draw needn't show every extreme that they name: `stiffness`: symmetric; every diagonal entry exceeds the sum of the magnitudes of the other entries of its row.
All inputs are finite; a program needn't handle non-finite values.
Results may differ from a plain program's by a relative error of at most 0.001.
Values sent between devices are 32-bit elements; how exact they have to be, the bound alone decides.
A program may use at most 64 MiB of HBM per device.

v0:
```python
import jax
import jax.numpy as jnp
from jax import lax
from jax.sharding import PartitionSpec as P

ITERS = 2


penalty = 0.15
epsilon = 1e-06
highest = lax.Precision.HIGHEST


def padded_2(block, sides, width):
    for axis, dim in sides:
        count = lax.axis_size(axis)
        forward = [(i, i + 1) for i in range(count - 1)]
        backward = [(target, source) for source, target in forward]
        low = lax.ppermute(
            lax.slice_in_dim(block, block.shape[dim] - width, None, axis=dim), axis, forward
        )
        high = lax.ppermute(lax.slice_in_dim(block, 0, width, axis=dim), axis, backward)
        block = jnp.concatenate([low, block, high], axis=dim)
    return block


def block_matrix(stiffness, size_c):
    points = stiffness.shape[0]
    cells = lax.broadcasted_iota(jnp.int32, (size_c, points), 0)
    slots = lax.broadcasted_iota(jnp.int32, (size_c, points), 1)
    selector = jnp.where(cells % points == slots, 1.0, 0.0).astype(jnp.float32)
    spread_out = jnp.dot(
        jnp.dot(selector, stiffness, precision=highest), selector.T, precision=highest
    )
    rows_block = lax.broadcasted_iota(jnp.int32, (size_c, size_c), 0) // points
    cols_block = lax.broadcasted_iota(jnp.int32, (size_c, size_c), 1) // points
    return jnp.where(rows_block == cols_block, spread_out, 0.0)


def stiffen(vector, stiffness, full_block):
    leading, size_a, size_b, size_c = vector.shape
    points = stiffness.shape[0]
    along_a = jnp.einsum(
        "ij,sajbc->saibc",
        stiffness,
        vector.reshape(leading, size_a // points, points, size_b, size_c),
        precision=highest,
    ).reshape(vector.shape)
    along_b = jnp.einsum(
        "ij,sabjc->sabic",
        stiffness,
        vector.reshape(leading, size_a, size_b // points, points, size_c),
        precision=highest,
    ).reshape(vector.shape)
    along_c = jnp.einsum("sabj,ij->sabi", vector, full_block, precision=highest)
    return along_a + along_b + along_c


def face_terms(vector, padded, points):
    accumulated = jnp.zeros_like(vector)
    neighbours = (
        (1, padded[:, 2:, 1:-1, 1:-1], padded[:, :-2, 1:-1, 1:-1]),
        (2, padded[:, 1:-1, 2:, 1:-1], padded[:, 1:-1, :-2, 1:-1]),
        (3, padded[:, 1:-1, 1:-1, 2:], padded[:, 1:-1, 1:-1, :-2]),
    )
    for axis_pos, higher, lower_side in neighbours:
        position = lax.broadcasted_iota(jnp.int32, vector.shape, axis_pos) % points
        accumulated = accumulated + jnp.where(position == points - 1, vector - higher, 0.0)
        accumulated = accumulated + jnp.where(position == 0, vector - lower_side, 0.0)
    return accumulated


def operate(vector, padded, diagonal, stiffness, full_block):
    return (
        diagonal * vector
        + stiffen(vector, stiffness, full_block)
        + penalty * face_terms(vector, padded, stiffness.shape[0])
    )


def per_solve(values):
    return values[:, None, None, None]


def on_device(rhs, basis, inertia, helm, stiffness):
    point_count = float(
        rhs[0].size * lax.axis_size("gx") * lax.axis_size("gy") * lax.axis_size("gz")
    )
    diagonal = helm[:, None, None, None] * inertia[None]
    full_block = block_matrix(stiffness, rhs.shape[3])

    def apply_all(vector):
        padded = padded_2(vector, (("gx", 1), ("gy", 2), ("gz", 3)), 1)
        return operate(vector, padded, diagonal, stiffness, full_block)

    def project(fields):
        return jnp.einsum("skxyz,sxyz->sk", basis, fields, precision=highest)

    def combine(weights):
        return jnp.einsum("sk,skxyz->sxyz", weights, basis, precision=highest)

    local_coef = project(rhs)
    local_gram = jnp.einsum("skxyz,slxyz->skl", basis, basis, preferred_element_type=jnp.float32)
    coef_sum, gram_sum = lax.psum((local_coef, local_gram), ("gx", "gy", "gz"))
    gram_matrix = gram_sum / point_count
    iterate = combine(coef_sum / point_count)
    residual = rhs - apply_all(iterate)
    direction = jnp.zeros_like(rhs)
    image_dir = jnp.zeros_like(rhs)
    norm_old = None
    step_old = None
    final_moment = None
    final_square = None
    for iteration in range(ITERS):
        image_vec = apply_all(residual)
        norm_part = jnp.sum(residual * residual, axis=(1, 2, 3))
        curv_part = jnp.sum(residual * image_vec, axis=(1, 2, 3))
        if iteration < ITERS - 1:
            norm_now, curvature = lax.psum((norm_part, curv_part), ("gx", "gy", "gz"))
        else:
            norm_now, curvature = lax.psum((norm_part, curv_part), ("gx", "gy", "gz"))
        if iteration == 0:
            conjugacy = jnp.zeros_like(norm_now)
            step_size = norm_now / curvature
        else:
            conjugacy = norm_now / norm_old
            step_size = norm_now / (curvature - conjugacy * norm_now / step_old)
        direction = residual + per_solve(conjugacy) * direction
        image_dir = image_vec + per_solve(conjugacy) * image_dir
        iterate = iterate + per_solve(step_size) * direction
        if iteration < ITERS - 1:
            residual = residual - per_solve(step_size) * image_dir
        norm_old = norm_now
        step_old = step_size
    final_moment, final_square = lax.psum(
        (project(iterate), jnp.sum(iterate * iterate, axis=(1, 2, 3))), ("gx", "gy", "gz")
    )
    weights = final_moment / point_count
    square = final_square / point_count
    spread = (
        square
        - 2.0 * jnp.sum(weights * weights, axis=1)
        + jnp.einsum("sk,skl,sl->s", weights, gram_matrix, weights, precision=highest)
    )
    remainder = iterate - combine(weights)
    new_basis = (remainder * per_solve(lax.rsqrt(spread + epsilon))).astype(jnp.bfloat16)
    return (iterate, new_basis)


def solution(mesh):
    placed = (
        P(None, "gx", "gy", "gz"),
        P(None, None, "gx", "gy", "gz"),
        P("gx", "gy", "gz"),
        P(),
        P(),
    )
    return jax.shard_map(
        on_device,
        mesh=mesh,
        in_specs=placed,
        out_specs=(P(None, "gx", "gy", "gz"), P(None, "gx", "gy", "gz")),
        check_vma=False,
    )
```

profile of v0, /device:TPU:0, one launch (start us, length us, event | category | flops | bytes accessed | tf_op | source)
XLA Modules:
  0.0 254.5 jit_solution(11118584132166019880)
XLA Ops:
  0.7 2.6 %fusion.20 = f32[4,1,8,1,1]{2,1,4,3,0:T(1,128)S(1)} fusion(f32[4,8,8,128,1]{3,4,2,1,0:T(1,128)} %bitcast.131, bf16[4,8,8,8,128]{4,3,2,1,0:T(8,128)(2,1)} %param.6), kind=kOutput, calls=%fused_computation.31 | convolution fusion | flops 3145728 | bytes 655488 | tf_op jit(solution)/shard_map/skxyz,sxyz->sk/dot_general | solution.py:97
  3.3 41.9 %psum.56 = f32[4,8]{1,0:T(4,128)S(1)} all-reduce(f32[4,8]{1,0:T(4,128)S(1)} %bitcast.130), channel_id=1, replica_groups=mesh['gx'=4,'gy'=4,'gz'=2] {'gx','gy','gz'}, use_global_device_ids=true, to_apply=%region_0.1 | all-reduce | flops 32 | bytes 256 | tf_op jit(solution)/shard_map/psum | solution.py:104
  46.0 1.3 collective-permute-start
  47.3 3.0 %collective-permute-start.1 = (f32[4,1,8,128]{3,1,2,0:T(1,128)S(1)}, f32[4,1,8,128]{3,1,2,0:T(1,128)S(1)}, u32[]{:S(2)}, u32[]{:S(2)}) collective-permute-start(f32[4,1,8,128]{3,1,2,0:T(1,128)S(1)} %get-tuple-element.39), channel_id=1, source_target_pairs={{0,8},{8,16},{16,24},{1,9},{9,17},{17,25},{2,10},{10,18},{18,26},{... | collective-permute-start | bytes 49160 | tf_op jit(solution)/shard_map/ppermute | solution.py:19
  51.6 1.3 collective-permute-start.2
  52.9 4.5 %collective-permute-start.3 = (f32[4,10,1,128]{3,1,2,0:T(8,128)S(1)}, f32[4,10,1,128]{3,1,2,0:T(8,128)S(1)}, u32[]{:S(2)}, u32[]{:S(2)}) collective-permute-start(f32[4,10,1,128]{3,1,2,0:T(8,128)S(1)} %get-tuple-element.33), channel_id=1, source_target_pairs={{0,2},{2,4},{4,6},{1,3},{3,5},{5,7},{8,10},{10,12},{12,14},{9,11},... | collective-permute-start | bytes 61448 | tf_op jit(solution)/shard_map/ppermute | solution.py:19
  57.5 1.6 collective-permute-done.3
  59.3 1.3 collective-permute-start.4
  60.6 4.6 %collective-permute-start.5 = (f32[4,10,10,1]{3,1,2,0:T(8,128)S(1)}, f32[4,10,10,1]{3,1,2,0:T(8,128)S(1)}, u32[]{:S(2)}, u32[]{:S(2)}) collective-permute-start(f32[4,10,10,1]{3,1,2,0:T(8,128)S(1)} %get-tuple-element.28), channel_id=1, source_target_pairs={{0,1},{2,3},{4,5},{6,7},{8,9},{10,11},{12,13},{14,15},{16,17},{18,... | collective-permute-start | bytes 4808 | tf_op jit(solution)/shard_map/ppermute | solution.py:19
  65.2 6.3 %collective-permute-done.4 = f32[4,10,10,1]{3,1,2,0:T(8,128)S(1)} collective-permute-done((f32[4,10,10,1]{3,1,2,0:T(8,128)S(1)}, f32[4,10,10,1]{3,1,2,0:T(8,128)S(1)}, u32[]{:S(2)}, u32[]{:S(2)}) %collective-permute-start.4) | collective-permute-done | bytes 1632 | tf_op jit(solution)/shard_map/ppermute | solution.py:22
  73.8 1.3 collective-permute-start.6
  75.1 3.0 %collective-permute-start.7 = (f32[4,1,8,128]{3,1,2,0:T(1,128)S(1)}, f32[4,1,8,128]{3,1,2,0:T(1,128)S(1)}, u32[]{:S(2)}, u32[]{:S(2)}) collective-permute-start(f32[4,1,8,128]{3,1,2,0:T(1,128)S(1)} %get-tuple-element.37), channel_id=1, source_target_pairs={{0,8},{8,16},{16,24},{1,9},{9,17},{17,25},{2,10},{10,18},{18,26},{... | collective-permute-start | bytes 49160 | tf_op jit(solution)/shard_map/ppermute | solution.py:19
  79.0 1.3 collective-permute-start.8
  80.3 4.6 %collective-permute-start.9 = (f32[4,10,1,128]{3,1,2,0:T(8,128)S(1)}, f32[4,10,1,128]{3,1,2,0:T(8,128)S(1)}, u32[]{:S(2)}, u32[]{:S(2)}) collective-permute-start(f32[4,10,1,128]{3,1,2,0:T(8,128)S(1)} %get-tuple-element.31), channel_id=1, source_target_pairs={{0,2},{2,4},{4,6},{1,3},{3,5},{5,7},{8,10},{10,12},{12,14},{9,11},... | collective-permute-start | bytes 61448 | tf_op jit(solution)/shard_map/ppermute | solution.py:19
  85.1 1.3 collective-permute-done.9
  86.7 1.3 collective-permute-start.10
  88.0 4.6 %collective-permute-start.11 = (f32[4,10,10,1]{3,1,2,0:T(8,128)S(1)}, f32[4,10,10,1]{3,1,2,0:T(8,128)S(1)}, u32[]{:S(2)}, u32[]{:S(2)}) collective-permute-start(f32[4,10,10,1]{3,1,2,0:T(8,128)S(1)} %get-tuple-element.26), channel_id=1, source_target_pairs={{0,1},{2,3},{4,5},{6,7},{8,9},{10,11},{12,13},{14,15},{16,17},{18,... | collective-permute-start | bytes 4808 | tf_op jit(solution)/shard_map/ppermute | solution.py:19
  92.8 5.2 %collective-permute-done.10 = f32[4,10,10,1]{3,1,2,0:T(8,128)S(1)} collective-permute-done((f32[4,10,10,1]{3,1,2,0:T(8,128)S(1)}, f32[4,10,10,1]{3,1,2,0:T(8,128)S(1)}, u32[]{:S(2)}, u32[]{:S(2)}) %collective-permute-start.10) | collective-permute-done | bytes 1632 | tf_op jit(solution)/shard_map/ppermute | solution.py:22
  98.0 1.2 collective-permute-done.11
  99.7 41.8 %all-reduce.2 = (f32[4]{0:T(128)S(1)}, f32[4]{0:T(128)S(1)}) all-reduce(f32[4]{0:T(128)S(1)} %get-tuple-element.7, f32[4]{0:T(128)S(1)} %get-tuple-element.6), channel_id=1, replica_groups=mesh['gx'=4,'gy'=4,'gz'=2] {'gx','gy','gz'}, use_global_device_ids=true, to_apply=%region_2.3 | all-reduce | flops 8 | bytes 64 | tf_op jit(solution)/shard_map/psum | solution.py:119
  141.7 1.3 collective-permute-start.12
  143.0 3.0 %collective-permute-start.13 = (f32[4,1,8,128]{3,1,2,0:T(1,128)S(1)}, f32[4,1,8,128]{3,1,2,0:T(1,128)S(1)}, u32[]{:S(2)}, u32[]{:S(2)}) collective-permute-start(f32[4,1,8,128]{3,1,2,0:T(1,128)S(1)} %get-tuple-element.35), channel_id=1, source_target_pairs={{0,8},{8,16},{16,24},{1,9},{9,17},{17,25},{2,10},{10,18},{18,26},{... | collective-permute-start | bytes 49160 | tf_op jit(solution)/shard_map/ppermute | solution.py:19
  146.9 1.3 collective-permute-start.14
  148.2 4.5 %collective-permute-start.15 = (f32[4,10,1,128]{3,1,2,0:T(8,128)S(1)}, f32[4,10,1,128]{3,1,2,0:T(8,128)S(1)}, u32[]{:S(2)}, u32[]{:S(2)}) collective-permute-start(f32[4,10,1,128]{3,1,2,0:T(8,128)S(1)} %get-tuple-element.29), channel_id=1, source_target_pairs={{0,2},{2,4},{4,6},{1,3},{3,5},{5,7},{8,10},{10,12},{12,14},{9,11},... | collective-permute-start | bytes 61448 | tf_op jit(solution)/shard_map/ppermute | solution.py:19
  153.0 1.3 collective-permute-done.15
  154.6 1.3 collective-permute-start.16
  155.9 4.6 %collective-permute-start.17 = (f32[4,10,10,1]{3,1,2,0:T(8,128)S(1)}, f32[4,10,10,1]{3,1,2,0:T(8,128)S(1)}, u32[]{:S(2)}, u32[]{:S(2)}) collective-permute-start(f32[4,10,10,1]{3,1,2,0:T(8,128)S(1)} %get-tuple-element.24), channel_id=1, source_target_pairs={{0,1},{2,3},{4,5},{6,7},{8,9},{10,11},{12,13},{14,15},{16,17},{18,... | collective-permute-start | bytes 4808 | tf_op jit(solution)/shard_map/ppermute | solution.py:19
  160.7 6.1 %collective-permute-done.16 = f32[4,10,10,1]{3,1,2,0:T(8,128)S(1)} collective-permute-done((f32[4,10,10,1]{3,1,2,0:T(8,128)S(1)}, f32[4,10,10,1]{3,1,2,0:T(8,128)S(1)}, u32[]{:S(2)}, u32[]{:S(2)}) %collective-permute-start.16) | collective-permute-done | bytes 1632 | tf_op jit(solution)/shard_map/ppermute | solution.py:22
  166.9 1.2 collective-permute-done.17
  168.5 41.5 %all-reduce.1 = (f32[4]{0:T(128)S(1)}, f32[4]{0:T(128)S(1)}) all-reduce(f32[4]{0:T(128)S(1)} %get-tuple-element.21, f32[4]{0:T(128)S(1)} %fusion.11), channel_id=1, replica_groups=mesh['gx'=4,'gy'=4,'gz'=2] {'gx','gy','gz'}, use_global_device_ids=true, to_apply=%region_6.7 | all-reduce | flops 8 | bytes 64 | tf_op jit(solution)/shard_map/psum | solution.py:121
  211.0 1.6 fusion.16
  212.6 40.1 %all-reduce = (f32[4,8]{1,0:T(4,128)S(1)}, f32[4,8,8]{2,1,0:T(8,128)S(1)}, f32[4]{0:T(128)S(1)}) all-reduce(f32[4,8]{1,0:T(4,128)S(1)} %bitcast.129, f32[4,8,8]{2,1,0:T(8,128)S(1)} %convolution_bitcast_fusion.3, f32[4]{0:T(128)S(1)} %get-tuple-element.17), channel_id=1, replica_groups=mesh['gx'=4,'gy'=4,'gz'=2] {'gx','gy','gz'}, use_global_device_ids=true, to_apply=%region_9.10 | all-reduce | flops 292 | bytes 2336 | tf_op jit(solution)/shard_map/psum | solution.py:135
  (66 shorter events, 11.4 us)
Async XLA Ops:
  0.6 49.8 %copy-start = (f32[8,8]{1,0:T(8,128)S(1)}, f32[8,8]{1,0:T(8,128)}, u32[]{:S(2)}) copy-start(f32[8,8]{1,0:T(8,128)} %param.9) | copy-start | bytes 772
  0.6 44.6 %copy-start.1 = (bf16[4,8,8,8,128]{4,3,2,1,0:T(8,128)(2,1)S(1)}, bf16[4,8,8,8,128]{4,3,2,1,0:T(8,128)(2,1)}, u32[]{:S(2)}) copy-start(bf16[4,8,8,8,128]{4,3,2,1,0:T(8,128)(2,1)} %param.6) | copy-start | bytes 1572868
  46.0 5.6 %collective-permute-start = (f32[4,1,8,128]{3,1,2,0:T(1,128)S(1)}, f32[4,1,8,128]{3,1,2,0:T(1,128)S(1)}, u32[]{:S(2)}, u32[]{:S(2)}) collective-permute-start(f32[4,1,8,128]{3,1,2,0:T(1,128)S(1)} %get-tuple-element.40), channel_id=1, source_target_pairs={{8,0},{16,8},{24,16},{9,1},{17,9},{25,17},{10,2},{18,10},{26,18},{... | collective-permute-start | bytes 49160 | tf_op jit(solution)/shard_map/ppermute | solution.py:22
  47.3 4.3 %collective-permute-start.1 = (f32[4,1,8,128]{3,1,2,0:T(1,128)S(1)}, f32[4,1,8,128]{3,1,2,0:T(1,128)S(1)}, u32[]{:S(2)}, u32[]{:S(2)}) collective-permute-start(f32[4,1,8,128]{3,1,2,0:T(1,128)S(1)} %get-tuple-element.39), channel_id=1, source_target_pairs={{0,8},{8,16},{16,24},{1,9},{9,17},{17,25},{2,10},{10,18},{18,26},{... | collective-permute-start | bytes 49160 | tf_op jit(solution)/shard_map/ppermute | solution.py:19
  51.6 5.9 %collective-permute-start.2 = (f32[4,10,1,128]{3,1,2,0:T(8,128)S(1)}, f32[4,10,1,128]{3,1,2,0:T(8,128)S(1)}, u32[]{:S(2)}, u32[]{:S(2)}) collective-permute-start(f32[4,10,1,128]{3,1,2,0:T(8,128)S(1)} %get-tuple-element.34), channel_id=1, source_target_pairs={{2,0},{4,2},{6,4},{3,1},{5,3},{7,5},{10,8},{12,10},{14,12},{11,9},... | collective-permute-start | bytes 61448 | tf_op jit(solution)/shard_map/ppermute | solution.py:22
  52.9 6.1 %collective-permute-start.3 = (f32[4,10,1,128]{3,1,2,0:T(8,128)S(1)}, f32[4,10,1,128]{3,1,2,0:T(8,128)S(1)}, u32[]{:S(2)}, u32[]{:S(2)}) collective-permute-start(f32[4,10,1,128]{3,1,2,0:T(8,128)S(1)} %get-tuple-element.33), channel_id=1, source_target_pairs={{0,2},{2,4},{4,6},{1,3},{3,5},{5,7},{8,10},{10,12},{12,14},{9,11},... | collective-permute-start | bytes 61448 | tf_op jit(solution)/shard_map/ppermute | solution.py:19
  59.1 6.1 %copy-start.2 = (f32[8,8,128]{2,1,0:T(8,128)S(1)}, f32[8,8,128]{2,1,0:T(8,128)}, u32[]{:S(2)}) copy-start(f32[8,8,128]{2,1,0:T(8,128)} %param.7) | copy-start | bytes 98308
  59.1 13.6 %copy-start.3 = (f32[4,8,8,128]{3,2,1,0:T(8,128)S(1)}, f32[4,8,8,128]{3,2,1,0:T(8,128)}, u32[]{:S(2)}) copy-start(f32[4,8,8,128]{3,2,1,0:T(8,128)} %param.5) | copy-start | bytes 393220
  59.3 12.3 %collective-permute-start.4 = (f32[4,10,10,1]{3,1,2,0:T(8,128)S(1)}, f32[4,10,10,1]{3,1,2,0:T(8,128)S(1)}, u32[]{:S(2)}, u32[]{:S(2)}) collective-permute-start(f32[4,10,10,1]{3,1,2,0:T(8,128)S(1)} %get-tuple-element.27), channel_id=1, source_target_pairs={{1,0},{3,2},{5,4},{7,6},{9,8},{11,10},{13,12},{15,14},{17,16},{19,... | collective-permute-start | bytes 4808 | tf_op jit(solution)/shard_map/ppermute | solution.py:22
  60.6 12.2 %collective-permute-start.5 = (f32[4,10,10,1]{3,1,2,0:T(8,128)S(1)}, f32[4,10,10,1]{3,1,2,0:T(8,128)S(1)}, u32[]{:S(2)}, u32[]{:S(2)}) collective-permute-start(f32[4,10,10,1]{3,1,2,0:T(8,128)S(1)} %get-tuple-element.28), channel_id=1, source_target_pairs={{0,1},{2,3},{4,5},{6,7},{8,9},{10,11},{12,13},{14,15},{16,17},{18,... | collective-permute-start | bytes 4808 | tf_op jit(solution)/shard_map/ppermute | solution.py:19
  72.7 0.7 copy-start.4
  73.8 4.3 %collective-permute-start.6 = (f32[4,1,8,128]{3,1,2,0:T(1,128)S(1)}, f32[4,1,8,128]{3,1,2,0:T(1,128)S(1)}, u32[]{:S(2)}, u32[]{:S(2)}) collective-permute-start(f32[4,1,8,128]{3,1,2,0:T(1,128)S(1)} %get-tuple-element.38), channel_id=1, source_target_pairs={{8,0},{16,8},{24,16},{9,1},{17,9},{25,17},{10,2},{18,10},{26,18},{... | collective-permute-start | bytes 49160 | tf_op jit(solution)/shard_map/ppermute | solution.py:22
  75.1 3.9 %collective-permute-start.7 = (f32[4,1,8,128]{3,1,2,0:T(1,128)S(1)}, f32[4,1,8,128]{3,1,2,0:T(1,128)S(1)}, u32[]{:S(2)}, u32[]{:S(2)}) collective-permute-start(f32[4,1,8,128]{3,1,2,0:T(1,128)S(1)} %get-tuple-element.37), channel_id=1, source_target_pairs={{0,8},{8,16},{16,24},{1,9},{9,17},{17,25},{2,10},{10,18},{18,26},{... | collective-permute-start | bytes 49160 | tf_op jit(solution)/shard_map/ppermute | solution.py:19
  79.0 6.1 %collective-permute-start.8 = (f32[4,10,1,128]{3,1,2,0:T(8,128)S(1)}, f32[4,10,1,128]{3,1,2,0:T(8,128)S(1)}, u32[]{:S(2)}, u32[]{:S(2)}) collective-permute-start(f32[4,10,1,128]{3,1,2,0:T(8,128)S(1)} %get-tuple-element.32), channel_id=1, source_target_pairs={{2,0},{4,2},{6,4},{3,1},{5,3},{7,5},{10,8},{12,10},{14,12},{11,9},... | collective-permute-start | bytes 61448 | tf_op jit(solution)/shard_map/ppermute | solution.py:22
  80.3 6.1 %collective-permute-start.9 = (f32[4,10,1,128]{3,1,2,0:T(8,128)S(1)}, f32[4,10,1,128]{3,1,2,0:T(8,128)S(1)}, u32[]{:S(2)}, u32[]{:S(2)}) collective-permute-start(f32[4,10,1,128]{3,1,2,0:T(8,128)S(1)} %get-tuple-element.31), channel_id=1, source_target_pairs={{0,2},{2,4},{4,6},{1,3},{3,5},{5,7},{8,10},{10,12},{12,14},{9,11},... | collective-permute-start | bytes 61448 | tf_op jit(solution)/shard_map/ppermute | solution.py:19
  86.7 11.4 %collective-permute-start.10 = (f32[4,10,10,1]{3,1,2,0:T(8,128)S(1)}, f32[4,10,10,1]{3,1,2,0:T(8,128)S(1)}, u32[]{:S(2)}, u32[]{:S(2)}) collective-permute-start(f32[4,10,10,1]{3,1,2,0:T(8,128)S(1)} %get-tuple-element.25), channel_id=1, source_target_pairs={{1,0},{3,2},{5,4},{7,6},{9,8},{11,10},{13,12},{15,14},{17,16},{19,... | collective-permute-start | bytes 4808 | tf_op jit(solution)/shard_map/ppermute | solution.py:22
  88.0 11.3 %collective-permute-start.11 = (f32[4,10,10,1]{3,1,2,0:T(8,128)S(1)}, f32[4,10,10,1]{3,1,2,0:T(8,128)S(1)}, u32[]{:S(2)}, u32[]{:S(2)}) collective-permute-start(f32[4,10,10,1]{3,1,2,0:T(8,128)S(1)} %get-tuple-element.26), channel_id=1, source_target_pairs={{0,1},{2,3},{4,5},{6,7},{8,9},{10,11},{12,13},{14,15},{16,17},{18,... | collective-permute-start | bytes 4808 | tf_op jit(solution)/shard_map/ppermute | solution.py:19
  141.7 4.9 %collective-permute-start.12 = (f32[4,1,8,128]{3,1,2,0:T(1,128)S(1)}, f32[4,1,8,128]{3,1,2,0:T(1,128)S(1)}, u32[]{:S(2)}, u32[]{:S(2)}) collective-permute-start(f32[4,1,8,128]{3,1,2,0:T(1,128)S(1)} %get-tuple-element.36), channel_id=1, source_target_pairs={{8,0},{16,8},{24,16},{9,1},{17,9},{25,17},{10,2},{18,10},{26,18},{... | collective-permute-start | bytes 49160 | tf_op jit(solution)/shard_map/ppermute | solution.py:22
  143.0 3.9 %collective-permute-start.13 = (f32[4,1,8,128]{3,1,2,0:T(1,128)S(1)}, f32[4,1,8,128]{3,1,2,0:T(1,128)S(1)}, u32[]{:S(2)}, u32[]{:S(2)}) collective-permute-start(f32[4,1,8,128]{3,1,2,0:T(1,128)S(1)} %get-tuple-element.35), channel_id=1, source_target_pairs={{0,8},{8,16},{16,24},{1,9},{9,17},{17,25},{2,10},{10,18},{18,26},{... | collective-permute-start | bytes 49160 | tf_op jit(solution)/shard_map/ppermute | solution.py:19
  146.9 6.1 %collective-permute-start.14 = (f32[4,10,1,128]{3,1,2,0:T(8,128)S(1)}, f32[4,10,1,128]{3,1,2,0:T(8,128)S(1)}, u32[]{:S(2)}, u32[]{:S(2)}) collective-permute-start(f32[4,10,1,128]{3,1,2,0:T(8,128)S(1)} %get-tuple-element.30), channel_id=1, source_target_pairs={{2,0},{4,2},{6,4},{3,1},{5,3},{7,5},{10,8},{12,10},{14,12},{11,9},... | collective-permute-start | bytes 61448 | tf_op jit(solution)/shard_map/ppermute | solution.py:22
  148.2 6.1 %collective-permute-start.15 = (f32[4,10,1,128]{3,1,2,0:T(8,128)S(1)}, f32[4,10,1,128]{3,1,2,0:T(8,128)S(1)}, u32[]{:S(2)}, u32[]{:S(2)}) collective-permute-start(f32[4,10,1,128]{3,1,2,0:T(8,128)S(1)} %get-tuple-element.29), channel_id=1, source_target_pairs={{0,2},{2,4},{4,6},{1,3},{3,5},{5,7},{8,10},{10,12},{12,14},{9,11},... | collective-permute-start | bytes 61448 | tf_op jit(solution)/shard_map/ppermute | solution.py:19
  154.6 12.3 %collective-permute-start.16 = (f32[4,10,10,1]{3,1,2,0:T(8,128)S(1)}, f32[4,10,10,1]{3,1,2,0:T(8,128)S(1)}, u32[]{:S(2)}, u32[]{:S(2)}) collective-permute-start(f32[4,10,10,1]{3,1,2,0:T(8,128)S(1)} %get-tuple-element.23), channel_id=1, source_target_pairs={{1,0},{3,2},{5,4},{7,6},{9,8},{11,10},{13,12},{15,14},{17,16},{19,... | collective-permute-start | bytes 4808 | tf_op jit(solution)/shard_map/ppermute | solution.py:22
  155.9 12.2 %collective-permute-start.17 = (f32[4,10,10,1]{3,1,2,0:T(8,128)S(1)}, f32[4,10,10,1]{3,1,2,0:T(8,128)S(1)}, u32[]{:S(2)}, u32[]{:S(2)}) collective-permute-start(f32[4,10,10,1]{3,1,2,0:T(8,128)S(1)} %get-tuple-element.24), channel_id=1, source_target_pairs={{0,1},{2,3},{4,5},{6,7},{8,9},{10,11},{12,13},{14,15},{16,17},{18,... | collective-permute-start | bytes 4808 | tf_op jit(solution)/shard_map/ppermute | solution.py:19
where the time goes:
time: 256 us; the launch traced here: 255 us
  blocking collectives  165 us (64%)
  starting transfers between devices  48.1 us (19%)
  waiting for transfers between devices  26.6 us (10%)
  matrix products  9.83 us (4%)
  local copies, waits for them, and re-layouts  2.59 us (1%)
    psum x2, blocking collectives, on_device(): norm_now, curvature = lax.psum((norm_part, curv_part), ('gx', 'gy', 'gz'))  83.3 us
    psum x1, blocking collectives, on_device(): coef_sum, gram_sum = lax.psum((local_coef, local_gram), ('gx', 'gy', 'gz'))  41.9 us
    psum x1, blocking collectives, on_device(): lax.psum((project(iterate), jnp.sum(iterate * iterate, axis=(1, 2, 3))),...  40.1 us
    ppermute x9, starting transfers between devices, padded_2(): lax.ppermute(lax.slice_in_dim(block, block.shape[dim] - width, None, axis...  36.5 us
    ppermute x9, waiting for transfers between devices, padded_2(): lax.ppermute(lax.slice_in_dim(block, 0, width, axis=dim), axis, backward)  17.7 us
    ppermute x9, starting transfers between devices, padded_2(): lax.ppermute(lax.slice_in_dim(block, 0, width, axis=dim), axis, backward)  11.6 us
    ppermute x9, waiting for transfers between devices, padded_2(): lax.ppermute(lax.slice_in_dim(block, block.shape[dim] - width, None, axis...  8.87 us
  transfers between devices with their start and end apart: 18, of which 11 were waited for; matrix products, arithmetic and copies ran while one was open for 1% of the time, Pallas kernels for 0%

commit v1 on v0

v1 whole, which is shorter than its diff:
```python
import functools

import jax
import jax.numpy as jnp
from jax import lax
from jax.experimental import pallas as pl
from jax.experimental.pallas import tpu as pltpu
from jax.sharding import PartitionSpec as P

penalty = 0.15
epsilon = 1e-06
highest = lax.Precision.HIGHEST
AXES = ("gx", "gy", "gz")
MESH = pl.DeviceIdType.MESH
LANES = 128
SUBLANES = 8
EXCHANGES = 3


def offsets(sizes):
    return [
        (a, b, c)
        for a in range(sizes[0])
        for b in range(sizes[1])
        for c in range(sizes[2])
        if a or b or c
    ]


def iota(shape, dim):
    return lax.broadcasted_iota(jnp.int32, shape, dim)


def line_matrix(stiffness, row, col):
    points = stiffness.shape[0]
    size = row.shape[0]
    picks = jnp.where(row[:, :1] % points == iota((size, points), 1), 1.0, 0.0)
    spread = jnp.dot(picks, stiffness, precision=highest, preferred_element_type=jnp.float32)
    spread = lax.dot_general(
        spread, picks, (((1,), (1,)), ((), ())), precision=highest,
        preferred_element_type=jnp.float32,
    )
    inside = jnp.where(row // points == col // points, spread, 0.0)
    first, last = row % points == 0, row % points == points - 1
    ends = jnp.where(first, penalty, 0.0) + jnp.where(last, penalty, 0.0)
    inside = inside + jnp.where(row == col, ends, 0.0)
    inside = inside - jnp.where((col == row + 1) & last, penalty, 0.0)
    return inside - jnp.where((col == row - 1) & first, penalty, 0.0)


def kernel(
    sizes, total_points,
    rhs, basis, inertia, helm, stiffness,
    sol, new,
    wide, x0, r0, q, mat_z, mat_xy,
    face_y, face_z, ghost_x, ghost_y, ghost_z,
    row1, rows2, got1, got2,
    halo_send, halo_recv, send1, recv1, send2, recv2,
):
    solves, keep, size_x, size_y, size_z = basis.shape
    here = tuple(lax.axis_index(axis) for axis in AXES)
    moves = offsets(sizes)
    unrolled = len(moves) <= 64
    inverse = 1.0 / total_points

    def partner(move):
        return {
            axis: lax.rem(here[d] + move[d], sizes[d]) for d, axis in enumerate(AXES)
        }

    def for_all(act):
        if unrolled:
            for slot, move in enumerate(moves):
                act(slot, partner(move))
        else:
            def step(index, carry):
                away = index + 1
                move = (
                    away // (sizes[1] * sizes[2]),
                    (away // sizes[2]) % sizes[1],
                    away % sizes[2],
                )
                act(index, partner(move))
                return carry
            lax.fori_loop(0, len(moves), step, 0)

    ghost_x[...] = jnp.zeros_like(ghost_x)
    ghost_y[...] = jnp.zeros_like(ghost_y)
    ghost_z[...] = jnp.zeros_like(ghost_z)
    barrier = pltpu.get_barrier_semaphore()
    for_all(
        lambda slot, target: pl.semaphore_signal(
            barrier, inc=1, device_id=target, device_id_type=MESH
        )
    )

    def row_of(parts):
        stack = jnp.concatenate([jnp.sum(part, axis=0, keepdims=True) for part in parts], axis=0)
        if len(parts) < LANES:
            stack = jnp.concatenate(
                [stack, jnp.zeros((LANES - len(parts), stack.shape[1]), jnp.float32)], axis=0
            )
        return lax.dot_general(
            jnp.ones((SUBLANES, stack.shape[1]), jnp.float32), stack,
            (((1,), (1,)), ((), ())), precision=highest, preferred_element_type=jnp.float32,
        )[:1]

    def inner(a, b):
        return jnp.sum(a * b, axis=0)

    def splat(row, lane):
        return jnp.broadcast_to(row[:, lane:lane + 1], (size_y, size_z))

    def send_all(source, got, send, recv):
        def act(slot, target):
            pltpu.make_async_remote_copy(
                src_ref=source, dst_ref=got.at[slot], send_sem=send, recv_sem=recv,
                device_id=target, device_id_type=MESH,
            ).start()
        for_all(act)

    def take_all(got, send, recv):
        pltpu.make_async_copy(got, got, send).wait()
        pltpu.make_async_copy(got, got, recv).wait()

    parts = []
    for s in range(solves):
        for k in range(keep):
            stored = basis[s, k].astype(jnp.float32)
            wide[s, k] = stored
            parts.append(inner(stored, rhs[s]))
    row1[...] = row_of(parts)
    pl.semaphore_wait(barrier, len(moves))
    send_all(row1, got1, send1, recv1)

    row, col = iota((size_z, size_z), 0), iota((size_z, size_z), 1)
    mat_z[...] = line_matrix(stiffness[...], row, col)
    area = size_x * size_y
    row, col = iota((area, area), 0), iota((area, area), 1)
    row_x, col_x, row_y, col_y = row // size_y, col // size_y, row % size_y, col % size_y
    mat_xy[...] = jnp.where(
        row_y == col_y, line_matrix(stiffness[...], row_x, col_x), 0.0
    ) + jnp.where(row_x == col_x, line_matrix(stiffness[...], row_y, col_y), 0.0)
    pairs = [(k, l) for k in range(keep) for l in range(k, keep)]
    gram = [inner(wide[s, k], wide[s, l]) for s in range(solves) for k, l in pairs]
    rows2[1:2] = row_of(gram[:LANES])
    gram_rest = gram[LANES:]

    lane = iota((size_y, size_z), 1)
    sub = iota((size_y, size_z), 0)

    def exchange(index, field):
        for s in range(solves):
            for side, pos in ((0, 0), (1, size_y - 1)):
                face_y[index, side, s] = jnp.concatenate(
                    [field[s, x, pos:pos + 1, :] for x in range(size_x)], axis=0
                )
        for side, pos in ((0, 0), (1, size_z - 1)):
            pack = jnp.zeros((size_y, size_z), jnp.float32)
            for s in range(solves):
                for x in range(size_x):
                    column = jnp.broadcast_to(field[s, x, :, pos:pos + 1], (size_y, size_z))
                    pack = jnp.where(lane == s * size_x + x, column, pack)
            face_z[index, side] = pack

        def each(act):
            for d, axis in enumerate(AXES):
                if sizes[d] == 1:
                    continue
                for side, step in ((0, -1), (1, 1)):
                    if d == 0:
                        source = field.at[:, 0 if side == 0 else size_x - 1]
                        target = ghost_x.at[index, 1 - side]
                    elif d == 1:
                        source, target = face_y.at[index, side], ghost_y.at[index, 1 - side]
                    else:
                        source, target = face_z.at[index, side], ghost_z.at[index, 1 - side]
                    sends = here[d] > 0 if side == 0 else here[d] < sizes[d] - 1
                    takes = here[d] < sizes[d] - 1 if side == 0 else here[d] > 0
                    copy = pltpu.make_async_remote_copy(
                        src_ref=source, dst_ref=target,
                        send_sem=halo_send.at[index, 2 * d + side],
                        recv_sem=halo_recv.at[index, 2 * d + side],
                        device_id={axis: jnp.clip(here[d] + step, 0, sizes[d] - 1)},
                        device_id_type=MESH,
                    )
                    act(copy, sends, takes)

        def start(copy, sends, takes):
            @pl.when(sends)
            def _():
                copy.start()

        def finish(copy, sends, takes):
            @pl.when(takes)
            def _():
                copy.wait_recv()

            @pl.when(sends)
            def _():
                copy.wait_send()

        each(start)
        return lambda: each(finish)

    def local(field, s):
        flat = field[s].reshape(area, size_z)
        along_z = jnp.dot(flat, mat_z[...], precision=highest, preferred_element_type=jnp.float32)
        along_xy = jnp.dot(mat_xy[...], flat, precision=highest, preferred_element_type=jnp.float32)
        out = (along_z + along_xy).reshape(size_x, size_y, size_z)
        return out + helm[s] * inertia[...] * field[s]

    def coupled(index, s):
        low_z, high_z = ghost_z[index, 0], ghost_z[index, 1]
        planes = []
        for x in range(size_x):
            spot = s * size_x + x
            plane = jnp.where(lane == 0, jnp.broadcast_to(low_z[:, spot:spot + 1], lane.shape), 0.0)
            plane = jnp.where(
                lane == size_z - 1, jnp.broadcast_to(high_z[:, spot:spot + 1], lane.shape), plane
            )
            plane = plane + jnp.where(
                sub == 0, jnp.broadcast_to(ghost_y[index, 0, s, x:x + 1, :], lane.shape), 0.0
            )
            plane = plane + jnp.where(
                sub == size_y - 1,
                jnp.broadcast_to(ghost_y[index, 1, s, x:x + 1, :], lane.shape), 0.0,
            )
            if x == 0:
                plane = plane + ghost_x[index, 0, s]
            if x == size_x - 1:
                plane = plane + ghost_x[index, 1, s]
            planes.append(plane)
        return penalty * jnp.stack(planes)

    take_all(got1, send1, recv1)
    coefs = (row1[...] + jnp.sum(got1[...], axis=0)) * inverse
    for s in range(solves):
        total = jnp.zeros((size_x, size_y, size_z), jnp.float32)
        for k in range(keep):
            total = total + splat(coefs, s * keep + k)[None] * wide[s, k]
        x0[s] = total
    finish = exchange(0, x0)
    for s in range(solves):
        r0[s] = rhs[s] - local(x0, s)
    finish()
    for s in range(solves):
        r0[s] = r0[s] + coupled(0, s)
    finish = exchange(1, r0)
    for s in range(solves):
        q[s] = local(r0, s)
    with_r = [inner(wide[s, k], r0[s]) for s in range(solves) for k in range(keep)]
    finish()
    for s in range(solves):
        q[s] = q[s] - coupled(1, s)
    finish = exchange(2, q)
    with_q = [inner(wide[s, k], q[s]) for s in range(solves) for k in range(keep)]
    moments = []
    for s in range(solves):
        moments.append(
            [inner(r0[s], r0[s]), inner(r0[s], q[s]), inner(q[s], q[s]), inner(q[s], local(q, s))]
        )
    finish()
    for s in range(solves):
        moments[s][3] = moments[s][3] - inner(q[s], coupled(2, s))
    flat_moments = [moments[s][j] for s in range(solves) for j in range(4)]
    rows2[0:1] = row_of(with_r + with_q + flat_moments + gram_rest)
    send_all(rows2, got2, send2, recv2)
    take_all(got2, send2, recv2)
    sums = (rows2[...] + jnp.sum(got2[...], axis=0)) * inverse
    main, other = sums[0:1], sums[1:2]
    at_q, at_m = solves * keep, 2 * solves * keep
    at_rest = at_m + 4 * solves

    for s in range(solves):
        coef = [splat(coefs, s * keep + k) for k in range(keep)]
        by_r = [splat(main, s * keep + k) for k in range(keep)]
        by_q = [splat(main, at_q + s * keep + k) for k in range(keep)]
        m0, m1, m2, m3 = (splat(main, at_m + 4 * s + j) for j in range(4))
        table = {}
        for at, (k, l) in enumerate(pairs):
            spot = s * len(pairs) + at
            value = splat(other, spot) if spot < LANES else splat(main, at_rest + spot - LANES)
            table[k, l] = table[l, k] = value
        first = m0 / m1
        middle = m2 / m1
        across = m3 / m1 - middle * middle
        flat = across <= 1e-6 * middle * middle
        second = jnp.where(flat, 0.0, (1.0 - first * middle) / jnp.where(flat, 1.0, across))
        on_q = second
        on_r = first - second * middle
        moved = [
            functools.reduce(lambda a, b: a + b, [table[k, l] * coef[l] for l in range(keep)])
            for k in range(keep)
        ]
        weight = [moved[k] + on_r * by_r[k] + on_q * by_q[k] for k in range(keep)]
        square = on_r * on_r * m0 + 2.0 * on_r * on_q * m1 + on_q * on_q * m2
        mixed = jnp.zeros_like(square)
        for k in range(keep):
            square = square + coef[k] * (2.0 * weight[k] - moved[k])
            pulled = functools.reduce(
                lambda a, b: a + b, [table[k, l] * weight[l] for l in range(keep)]
            )
            mixed = mixed + weight[k] * (pulled - 2.0 * weight[k])
        scale = lax.rsqrt(square + mixed + epsilon)
        answer = x0[s] + on_r[None] * r0[s] + on_q[None] * q[s]
        sol[s] = answer
        for k in range(keep):
            answer = answer - weight[k][None] * wide[s, k]
        new[s] = (answer * scale[None]).astype(jnp.bfloat16)


def on_device(sizes, rhs, basis, inertia, helm, stiffness):
    solves, size_x, size_y, size_z = rhs.shape
    total_points = float(rhs[0].size * sizes[0] * sizes[1] * sizes[2])
    others = sizes[0] * sizes[1] * sizes[2] - 1
    field = pltpu.VMEM(rhs.shape, jnp.float32)
    vmem = pl.BlockSpec(memory_space=pltpu.VMEM)
    smem = pl.BlockSpec(memory_space=pltpu.SMEM)
    area = size_x * size_y
    faces = (EXCHANGES, 2, solves)
    return pl.pallas_call(
        functools.partial(kernel, sizes, total_points),
        out_shape=(
            jax.ShapeDtypeStruct(rhs.shape, jnp.float32),
            jax.ShapeDtypeStruct(rhs.shape, jnp.bfloat16),
        ),
        in_specs=[vmem, vmem, vmem, smem, vmem],
        out_specs=(vmem, vmem),
        scratch_shapes=[
            pltpu.VMEM(basis.shape, jnp.float32),
            field, field, field,
            pltpu.VMEM((size_z, size_z), jnp.float32),
            pltpu.VMEM((area, area), jnp.float32),
            pltpu.VMEM((*faces, size_x, size_z), jnp.float32),
            pltpu.VMEM((EXCHANGES, 2, size_y, size_z), jnp.float32),
            pltpu.VMEM((*faces, size_y, size_z), jnp.float32),
            pltpu.VMEM((*faces, size_x, size_z), jnp.float32),
            pltpu.VMEM((EXCHANGES, 2, size_y, size_z), jnp.float32),
            pltpu.VMEM((1, LANES), jnp.float32),
            pltpu.VMEM((2, LANES), jnp.float32),
            pltpu.VMEM((others, 1, LANES), jnp.float32),
            pltpu.VMEM((others, 2, LANES), jnp.float32),
            pltpu.SemaphoreType.DMA((EXCHANGES, 6)),
            pltpu.SemaphoreType.DMA((EXCHANGES, 6)),
            pltpu.SemaphoreType.DMA,
            pltpu.SemaphoreType.DMA,
            pltpu.SemaphoreType.DMA,
            pltpu.SemaphoreType.DMA,
        ],
        compiler_params=pltpu.CompilerParams(collective_id=0, has_side_effects=True),
    )(rhs, basis, inertia, helm, stiffness)


def solution(mesh):
    placed = (
        P(None, "gx", "gy", "gz"),
        P(None, None, "gx", "gy", "gz"),
        P("gx", "gy", "gz"),
        P(),
        P(),
    )
    sizes = tuple(mesh.shape[axis] for axis in AXES)
    return jax.shard_map(
        functools.partial(on_device, sizes),
        mesh=mesh,
        in_specs=placed,
        out_specs=(P(None, "gx", "gy", "gz"), P(None, "gx", "gy", "gz")),
        check_vma=False,
    )
```

time: 256 us -> 31.1 us (0.12)
  blocking collectives: 165 us -> 0 us
  starting transfers between devices: 48.1 us -> 0 us
  Pallas kernels: 0 us -> 28 us
  waiting for transfers between devices: 26.6 us -> 0 us
  matrix products: 9.83 us -> 0 us
    psum x4 -> x0, blocking collectives: 165 us -> none  [the longest x2 83.3 us: on_device(): norm_now, curvature = lax.psum((norm_part, curv_part), ('gx', 'gy', 'gz'))]
    ppermute x18 -> x0, starting transfers between devices: 48.1 us -> none  [the longest x9 36.5 us: padded_2(): lax.ppermute(lax.slice_in_dim(block, block.shape[dim] - width, None, axis...]
    pallas_call x0 -> x1, Pallas kernels: none -> 28 us  [on_device(): pl.pallas_call(functools.partial(kernel, sizes, total_points), out_shape=...]
    ppermute x18 -> x0, waiting for transfers between devices: 26.6 us -> none  [the longest x9 17.7 us: padded_2(): lax.ppermute(lax.slice_in_dim(block, 0, width, axis=dim), axis, backward)]
    dot_general x17 -> x0, matrix products: 9.83 us -> none  [the longest x2 4.23 us: project(): return jnp.einsum('skxyz,sxyz->sk', basis, fields, precision=highest)]
  transfers between devices with their start and end apart: 18 -> 0, of which waited for: 11 -> 0; matrix products, arithmetic and copies ran while one was open for 1% -> 0% of each run, Pallas kernels for 0% -> 0%
where the time goes in v1:
time: 31.1 us; the launch traced here: 30.9 us
  Pallas kernels  28 us (90%)
  local copies, waits for them, and re-layouts  2.23 us (7%)
  between operations  0.65 us (2%)
    pallas_call x1, Pallas kernels, on_device(): pl.pallas_call(functools.partial(kernel, sizes, total_points), out_shape=...  28 us
    unnamed x4, local copies, waits for them, and re-layouts  2.23 us

profile of v1, /device:TPU:0, one launch (start us, length us, event | category | flops | bytes accessed | tf_op | source)
XLA Modules:
  0.0 30.9 jit_solution(13049838903748836665)
XLA Ops:
  0.6 28.0 %shard_map.68 = (f32[4,8,8,128]{3,2,1,0:T(8,128)}, bf16[4,8,8,128]{3,2,1,0:T(8,128)(2,1)}) custom-call(f32[4,8,8,128]{3,2,1,0:T(8,128)} %rhs.1, bf16[4,8,8,8,128]{4,3,2,1,0:T(8,128)(2,1)} %basis.1, f32[8,8,128]{2,1,0:T(8,128)} %inertia.1, f32[4]{0:T(128)} %helm.1, f32[8,8]{1,0:T(8,128)} %stiffness.1), custom_call_target="tpu_custom_call" | custom-call | tf_op jit(solution)/shard_map/pallas_call | solution.py:322
  28.7 0.0 copy-start
  28.7 1.6 %copy.9 = f32[4,8,8,128]{3,2,1,0:T(8,128)} copy(f32[4,8,8,128]{3,2,1,0:T(8,128)} %get-tuple-element.4) | data formatting | bytes 262144
  30.3 0.0 copy-done
  30.3 0.6 %copy.10 = bf16[4,8,8,128]{3,2,1,0:T(8,128)(2,1)} copy(bf16[4,8,8,128]{3,2,1,0:T(8,128)(2,1)S(1)} %copy-done) | data formatting | bytes 131072
Async XLA Ops:
  28.7 1.6 %copy-start = (bf16[4,8,8,128]{3,2,1,0:T(8,128)(2,1)S(1)}, bf16[4,8,8,128]{3,2,1,0:T(8,128)(2,1)}, u32[]{:S(2)}) copy-start(bf16[4,8,8,128]{3,2,1,0:T(8,128)(2,1)} %get-tuple-element.5) | copy-start | bytes 196612

commit v2 on v1

--- a/solution.py
+++ b/solution.py
@@ -50,8 +50,9 @@
 
 def kernel(
     sizes, total_points,
-    rhs, basis, inertia, helm, stiffness,
+    rhs_any, basis_any, inertia_any, helm, stiffness_any,
     sol, new,
+    rhs, basis, inertia, stiffness, load_sem,
     wide, x0, r0, q, mat_z, mat_xy,
     face_y, face_z, ghost_x, ghost_y, ghost_z,
     row1, rows2, got1, got2,
@@ -84,6 +85,17 @@
                 return carry
             lax.fori_loop(0, len(moves), step, 0)
 
+    loads = [
+        pltpu.make_async_copy(source, target, load_sem.at[at])
+        for at, (source, target) in enumerate(
+            (
+                (rhs_any, rhs), (basis_any, basis),
+                (inertia_any, inertia), (stiffness_any, stiffness),
+            )
+        )
+    ]
+    for load in loads:
+        load.start()
     ghost_x[...] = jnp.zeros_like(ghost_x)
     ghost_y[...] = jnp.zeros_like(ghost_y)
     ghost_z[...] = jnp.zeros_like(ghost_z)
@@ -124,6 +136,8 @@
         pltpu.make_async_copy(got, got, recv).wait()
 
     parts = []
+    for load in loads:
+        load.wait()
     for s in range(solves):
         for k in range(keep):
             stored = basis[s, k].astype(jnp.float32)
@@ -307,7 +321,12 @@
         sol[s] = answer
         for k in range(keep):
             answer = answer - weight[k][None] * wide[s, k]
-        new[s] = (answer * scale[None]).astype(jnp.bfloat16)
+        new[s] = answer * scale[None]
+
+
+def write(sol_in, new_in, sol, new):
+    sol[...] = sol_in[...]
+    new[...] = new_in[...].astype(jnp.bfloat16)
 
 
 def on_device(sizes, rhs, basis, inertia, helm, stiffness):
@@ -319,15 +338,18 @@
     smem = pl.BlockSpec(memory_space=pltpu.SMEM)
     area = size_x * size_y
     faces = (EXCHANGES, 2, solves)
-    return pl.pallas_call(
+    anywhere = pl.BlockSpec(memory_space=pl.ANY)
+    held = pl.pallas_call(
         functools.partial(kernel, sizes, total_points),
-        out_shape=(
-            jax.ShapeDtypeStruct(rhs.shape, jnp.float32),
-            jax.ShapeDtypeStruct(rhs.shape, jnp.bfloat16),
-        ),
-        in_specs=[vmem, vmem, vmem, smem, vmem],
+        out_shape=(field, field),
+        in_specs=[anywhere, anywhere, anywhere, smem, anywhere],
         out_specs=(vmem, vmem),
         scratch_shapes=[
+            field,
+            pltpu.VMEM(basis.shape, basis.dtype),
+            pltpu.VMEM(inertia.shape, inertia.dtype),
+            pltpu.VMEM(stiffness.shape, stiffness.dtype),
+            pltpu.SemaphoreType.DMA((4,)),
             pltpu.VMEM(basis.shape, jnp.float32),
             field, field, field,
             pltpu.VMEM((size_z, size_z), jnp.float32),
@@ -350,6 +372,15 @@
         ],
         compiler_params=pltpu.CompilerParams(collective_id=0, has_side_effects=True),
     )(rhs, basis, inertia, helm, stiffness)
+    return pl.pallas_call(
+        write,
+        out_shape=(
+            jax.ShapeDtypeStruct(rhs.shape, jnp.float32),
+            jax.ShapeDtypeStruct(rhs.shape, jnp.bfloat16),
+        ),
+        in_specs=[vmem, vmem],
+        out_specs=(vmem, vmem),
+    )(*(pltpu.with_memory_space_constraint(part, pltpu.VMEM) for part in held))
 
 
 def solution(mesh):

time: 31.1 us -> 28.5 us (0.916)
  local copies, waits for them, and re-layouts: 2.23 us -> 0 us
    unnamed x4 -> x0, local copies, waits for them, and re-layouts: 2.23 us -> none
    pallas_call x1, Pallas kernels: 28 us -> 27 us  [on_device(): pl.pallas_call(functools.partial(kernel, sizes, total_points), out_shape=...]
    pallas_call x0 -> x1, Pallas kernels: none -> 0.69 us  [on_device(): pl.pallas_call(write, out_shape=(jax.ShapeDtypeStruct(rhs.shape, jnp.floa...]
where the time goes in v2:
time: 28.5 us; the launch traced here: 28.4 us
  Pallas kernels  27.7 us (97%)
  between operations  0.64 us (2%)
    pallas_call x1, Pallas kernels, on_device(): pl.pallas_call(functools.partial(kernel, sizes, total_points), out_shape=...  27 us
    pallas_call x1, Pallas kernels, on_device(): pl.pallas_call(write, out_shape=(jax.ShapeDtypeStruct(rhs.shape, jnp.floa...  0.69 us

profile of v2, /device:TPU:0, one launch (start us, length us, event | category | flops | bytes accessed | tf_op | source)
XLA Modules:
  0.0 28.4 jit_solution(9659314529181960416)
XLA Ops:
  0.6 27.0 %shard_map.68 = (f32[4,8,8,128]{3,2,1,0:T(8,128)S(1)}, f32[4,8,8,128]{3,2,1,0:T(8,128)S(1)}) custom-call(f32[4,8,8,128]{3,2,1,0:T(8,128)} %rhs_any.1, bf16[4,8,8,8,128]{4,3,2,1,0:T(8,128)(2,1)} %basis_any.1, f32[8,8,128]{2,1,0:T(8,128)} %inertia_any.1, f32[4]{0:T(128)} %helm.1, f32[8,8]{1,0:T(8,128)} %stiffness_any.1), custom_call_target="tpu_custom_call" | custom-call | tf_op jit(solution)/shard_map/pallas_call | solution.py:342
  27.7 0.7 %shard_map.69 = (f32[4,8,8,128]{3,2,1,0:T(8,128)}, bf16[4,8,8,128]{3,2,1,0:T(8,128)(2,1)}) custom-call(f32[4,8,8,128]{3,2,1,0:T(8,128)S(1)} %get-tuple-element.4.sol_in, f32[4,8,8,128]{3,2,1,0:T(8,128)S(1)} %get-tuple-element.5.new_in), custom_call_target="tpu_custom_call" | custom-call | tf_op jit(solution)/shard_map/pallas_call | solution.py:375

commit v3 on v2

--- a/solution.py
+++ b/solution.py
@@ -14,7 +14,7 @@
 MESH = pl.DeviceIdType.MESH
 LANES = 128
 SUBLANES = 8
-EXCHANGES = 3
+EXCHANGES = 2
 
 
 def offsets(sizes):
@@ -55,6 +55,7 @@
     rhs, basis, inertia, stiffness, load_sem,
     wide, x0, r0, q, mat_z, mat_xy,
     face_y, face_z, ghost_x, ghost_y, ghost_z,
+    many_face_y, many_face_z, many_x, many_y, many_z,
     row1, rows2, got1, got2,
     halo_send, halo_recv, send1, recv1, send2, recv2,
 ):
@@ -96,9 +97,8 @@
     ]
     for load in loads:
         load.start()
-    ghost_x[...] = jnp.zeros_like(ghost_x)
-    ghost_y[...] = jnp.zeros_like(ghost_y)
-    ghost_z[...] = jnp.zeros_like(ghost_z)
+    for ghost in (ghost_x, ghost_y, ghost_z, many_x, many_y, many_z):
+        ghost[...] = jnp.zeros_like(ghost)
     barrier = pltpu.get_barrier_semaphore()
     for_all(
         lambda slot, target: pl.semaphore_signal(
@@ -135,6 +135,51 @@
         pltpu.make_async_copy(got, got, send).wait()
         pltpu.make_async_copy(got, got, recv).wait()
 
+    lane = iota((size_y, size_z), 1)
+    sub = iota((size_y, size_z), 0)
+
+    def column_pack(plane_of, pos):
+        pack = jnp.zeros((size_y, size_z), jnp.float32)
+        for s in range(solves):
+            for x in range(size_x):
+                column = jnp.broadcast_to(plane_of(s, x)[:, pos:pos + 1], (size_y, size_z))
+                pack = jnp.where(lane == s * size_x + x, column, pack)
+        return pack
+
+    def trade(index, source, target):
+        def each(act):
+            for d, axis in enumerate(AXES):
+                if sizes[d] == 1:
+                    continue
+                for side, step in ((0, -1), (1, 1)):
+                    sends = here[d] > 0 if side == 0 else here[d] < sizes[d] - 1
+                    takes = here[d] < sizes[d] - 1 if side == 0 else here[d] > 0
+                    copy = pltpu.make_async_remote_copy(
+                        src_ref=source(d, side), dst_ref=target(d, 1 - side),
+                        send_sem=halo_send.at[index, 2 * d + side],
+                        recv_sem=halo_recv.at[index, 2 * d + side],
+                        device_id={axis: jnp.clip(here[d] + step, 0, sizes[d] - 1)},
+                        device_id_type=MESH,
+                    )
+                    act(copy, sends, takes)
+
+        def start(copy, sends, takes):
+            @pl.when(sends)
+            def _():
+                copy.start()
+
+        def finish(copy, sends, takes):
+            @pl.when(takes)
+            def _():
+                copy.wait_recv()
+
+            @pl.when(sends)
+            def _():
+                copy.wait_send()
+
+        each(start)
+        return lambda: each(finish)
+
     parts = []
     for load in loads:
         load.wait()
@@ -144,8 +189,24 @@
             wide[s, k] = stored
             parts.append(inner(stored, rhs[s]))
     row1[...] = row_of(parts)
+    ends_x, ends_y, ends_z = ((0, size - 1) for size in (size_x, size_y, size_z))
+    for k in range(keep):
+        for side in (0, 1):
+            for s in range(solves):
+                many_face_y[side, s, k] = jnp.concatenate(
+                    [wide[s, k, x, ends_y[side]:ends_y[side] + 1, :] for x in range(size_x)],
+                    axis=0,
+                )
+            many_face_z[side, k] = column_pack(lambda s, x: wide[s, k, x], ends_z[side])
     pl.semaphore_wait(barrier, len(moves))
     send_all(row1, got1, send1, recv1)
+    finish_many = trade(
+        0,
+        lambda d, side: (
+            wide.at[:, :, ends_x[side]], many_face_y.at[side], many_face_z.at[side]
+        )[d],
+        lambda d, side: (many_x, many_y, many_z)[d].at[side],
+    )
 
     row, col = iota((size_z, size_z), 0), iota((size_z, size_z), 1)
     mat_z[...] = line_matrix(stiffness[...], row, col)
@@ -160,9 +221,6 @@
     rows2[1:2] = row_of(gram[:LANES])
     gram_rest = gram[LANES:]
 
-    lane = iota((size_y, size_z), 1)
-    sub = iota((size_y, size_z), 0)
-
     def exchange(index, field):
         for s in range(solves):
             for side, pos in ((0, 0), (1, size_y - 1)):
@@ -170,52 +228,14 @@
                     [field[s, x, pos:pos + 1, :] for x in range(size_x)], axis=0
                 )
         for side, pos in ((0, 0), (1, size_z - 1)):
-            pack = jnp.zeros((size_y, size_z), jnp.float32)
-            for s in range(solves):
-                for x in range(size_x):
-                    column = jnp.broadcast_to(field[s, x, :, pos:pos + 1], (size_y, size_z))
-                    pack = jnp.where(lane == s * size_x + x, column, pack)
-            face_z[index, side] = pack
-
-        def each(act):
-            for d, axis in enumerate(AXES):
-                if sizes[d] == 1:
-                    continue
-                for side, step in ((0, -1), (1, 1)):
-                    if d == 0:
-                        source = field.at[:, 0 if side == 0 else size_x - 1]
-                        target = ghost_x.at[index, 1 - side]
-                    elif d == 1:
-                        source, target = face_y.at[index, side], ghost_y.at[index, 1 - side]
-                    else:
-                        source, target = face_z.at[index, side], ghost_z.at[index, 1 - side]
-                    sends = here[d] > 0 if side == 0 else here[d] < sizes[d] - 1
-                    takes = here[d] < sizes[d] - 1 if side == 0 else here[d] > 0
-                    copy = pltpu.make_async_remote_copy(
-                        src_ref=source, dst_ref=target,
-                        send_sem=halo_send.at[index, 2 * d + side],
-                        recv_sem=halo_recv.at[index, 2 * d + side],
-                        device_id={axis: jnp.clip(here[d] + step, 0, sizes[d] - 1)},
-                        device_id_type=MESH,
-                    )
-                    act(copy, sends, takes)
-
-        def start(copy, sends, takes):
-            @pl.when(sends)
-            def _():
-                copy.start()
-
-        def finish(copy, sends, takes):
-            @pl.when(takes)
-            def _():
-                copy.wait_recv()
-
-            @pl.when(sends)
-            def _():
-                copy.wait_send()
-
-        each(start)
-        return lambda: each(finish)
+            face_z[index, side] = column_pack(lambda s, x: field[s, x], pos)
+        return trade(
+            1 + index,
+            lambda d, side: (
+                field.at[:, ends_x[side]], face_y.at[index, side], face_z.at[index, side]
+            )[d],
+            lambda d, side: (ghost_x, ghost_y, ghost_z)[d].at[index, side],
+        )
 
     def local(field, s):
         flat = field[s].reshape(area, size_z)
@@ -224,8 +244,9 @@
         out = (along_z + along_xy).reshape(size_x, size_y, size_z)
         return out + helm[s] * inertia[...] * field[s]
 
-    def coupled(index, s):
-        low_z, high_z = ghost_z[index, 0], ghost_z[index, 1]
+    def coupled(s, ghost_x, ghost_y, ghost_z):
+        low_z, high_z = ghost_z(0), ghost_z(1)
+        low_y, high_y = ghost_y(0, s), ghost_y(1, s)
         planes = []
         for x in range(size_x):
             spot = s * size_x + x
@@ -234,40 +255,66 @@
                 lane == size_z - 1, jnp.broadcast_to(high_z[:, spot:spot + 1], lane.shape), plane
             )
             plane = plane + jnp.where(
-                sub == 0, jnp.broadcast_to(ghost_y[index, 0, s, x:x + 1, :], lane.shape), 0.0
+                sub == 0, jnp.broadcast_to(low_y[x:x + 1, :], lane.shape), 0.0
             )
             plane = plane + jnp.where(
                 sub == size_y - 1,
-                jnp.broadcast_to(ghost_y[index, 1, s, x:x + 1, :], lane.shape), 0.0,
+                jnp.broadcast_to(high_y[x:x + 1, :], lane.shape), 0.0,
             )
             if x == 0:
-                plane = plane + ghost_x[index, 0, s]
+                plane = plane + ghost_x(0, s)
             if x == size_x - 1:
-                plane = plane + ghost_x[index, 1, s]
+                plane = plane + ghost_x(1, s)
             planes.append(plane)
         return penalty * jnp.stack(planes)
 
+    def received(index, s):
+        return coupled(
+            s,
+            lambda side, at: ghost_x[index, side, at],
+            lambda side, at: ghost_y[index, side, at],
+            lambda side: ghost_z[index, side],
+        )
+
     take_all(got1, send1, recv1)
     coefs = (row1[...] + jnp.sum(got1[...], axis=0)) * inverse
+    splats = [[splat(coefs, s * keep + k) for k in range(keep)] for s in range(solves)]
     for s in range(solves):
         total = jnp.zeros((size_x, size_y, size_z), jnp.float32)
         for k in range(keep):
-            total = total + splat(coefs, s * keep + k)[None] * wide[s, k]
+            total = total + splats[s][k][None] * wide[s, k]
         x0[s] = total
-    finish = exchange(0, x0)
     for s in range(solves):
         r0[s] = rhs[s] - local(x0, s)
-    finish()
-    for s in range(solves):
-        r0[s] = r0[s] + coupled(0, s)
-    finish = exchange(1, r0)
+    by_lane = []
+    for k in range(keep):
+        mixed = jnp.zeros((size_y, size_z), jnp.float32)
+        for s in range(solves):
+            mixed = jnp.where(lane // size_x == s, splats[s][k], mixed)
+        by_lane.append(mixed)
+    finish_many()
+
+    def combined(values):
+        return functools.reduce(lambda a, b: a + b, values)
+
+    both_z = [
+        combined([by_lane[k] * many_z[side, k] for k in range(keep)]) for side in (0, 1)
+    ]
+    for s in range(solves):
+        r0[s] = r0[s] + coupled(
+            s,
+            lambda side, at: combined([splats[at][k] * many_x[side, at, k] for k in range(keep)]),
+            lambda side, at: combined([splats[at][k] * many_y[side, at, k] for k in range(keep)]),
+            lambda side: both_z[side],
+        )
+    finish = exchange(0, r0)
     for s in range(solves):
         q[s] = local(r0, s)
     with_r = [inner(wide[s, k], r0[s]) for s in range(solves) for k in range(keep)]
     finish()
     for s in range(solves):
-        q[s] = q[s] - coupled(1, s)
-    finish = exchange(2, q)
+        q[s] = q[s] - received(0, s)
+    finish = exchange(1, q)
     with_q = [inner(wide[s, k], q[s]) for s in range(solves) for k in range(keep)]
     moments = []
     for s in range(solves):
@@ -276,7 +323,7 @@
         )
     finish()
     for s in range(solves):
-        moments[s][3] = moments[s][3] - inner(q[s], coupled(2, s))
+        moments[s][3] = moments[s][3] - inner(q[s], received(1, s))
     flat_moments = [moments[s][j] for s in range(solves) for j in range(4)]
     rows2[0:1] = row_of(with_r + with_q + flat_moments + gram_rest)
     send_all(rows2, got2, send2, recv2)
@@ -331,6 +378,7 @@
 
 def on_device(sizes, rhs, basis, inertia, helm, stiffness):
     solves, size_x, size_y, size_z = rhs.shape
+    keep = basis.shape[1]
     total_points = float(rhs[0].size * sizes[0] * sizes[1] * sizes[2])
     others = sizes[0] * sizes[1] * sizes[2] - 1
     field = pltpu.VMEM(rhs.shape, jnp.float32)
@@ -359,12 +407,17 @@
             pltpu.VMEM((*faces, size_y, size_z), jnp.float32),
             pltpu.VMEM((*faces, size_x, size_z), jnp.float32),
             pltpu.VMEM((EXCHANGES, 2, size_y, size_z), jnp.float32),
+            pltpu.VMEM((2, solves, keep, size_x, size_z), jnp.float32),
+            pltpu.VMEM((2, keep, size_y, size_z), jnp.float32),
+            pltpu.VMEM((2, solves, keep, size_y, size_z), jnp.float32),
+            pltpu.VMEM((2, solves, keep, size_x, size_z), jnp.float32),
+            pltpu.VMEM((2, keep, size_y, size_z), jnp.float32),
             pltpu.VMEM((1, LANES), jnp.float32),
             pltpu.VMEM((2, LANES), jnp.float32),
             pltpu.VMEM((others, 1, LANES), jnp.float32),
             pltpu.VMEM((others, 2, LANES), jnp.float32),
-            pltpu.SemaphoreType.DMA((EXCHANGES, 6)),
-            pltpu.SemaphoreType.DMA((EXCHANGES, 6)),
+            pltpu.SemaphoreType.DMA((1 + EXCHANGES, 6)),
+            pltpu.SemaphoreType.DMA((1 + EXCHANGES, 6)),
             pltpu.SemaphoreType.DMA,
             pltpu.SemaphoreType.DMA,
             pltpu.SemaphoreType.DMA,

time: 28.5 us -> 26.5 us (0.930)
  Pallas kernels: 27.7 us -> 25.7 us
    pallas_call x1, Pallas kernels: 27 us -> 25 us  [on_device(): pl.pallas_call(functools.partial(kernel, sizes, total_points), out_shape=...]
where the time goes in v3:
time: 26.5 us; the launch traced here: 26.3 us
  Pallas kernels  25.7 us (97%)
  between operations  0.64 us (2%)
    pallas_call x1, Pallas kernels, on_device(): pl.pallas_call(functools.partial(kernel, sizes, total_points), out_shape=...  25 us
    pallas_call x1, Pallas kernels, on_device(): pl.pallas_call(write, out_shape=(jax.ShapeDtypeStruct(rhs.shape, jnp.floa...  0.69 us

profile of v3, /device:TPU:0, one launch (start us, length us, event | category | flops | bytes accessed | tf_op | source)
XLA Modules:
  0.0 26.3 jit_solution(4166778445946923092)
XLA Ops:
  0.6 25.0 %shard_map.68 = (f32[4,8,8,128]{3,2,1,0:T(8,128)S(1)}, f32[4,8,8,128]{3,2,1,0:T(8,128)S(1)}) custom-call(f32[4,8,8,128]{3,2,1,0:T(8,128)} %rhs_any.1, bf16[4,8,8,8,128]{4,3,2,1,0:T(8,128)(2,1)} %basis_any.1, f32[8,8,128]{2,1,0:T(8,128)} %inertia_any.1, f32[4]{0:T(128)} %helm.1, f32[8,8]{1,0:T(8,128)} %stiffness_any.1), custom_call_target="tpu_custom_call" | custom-call | tf_op jit(solution)/shard_map/pallas_call | solution.py:390
  25.6 0.7 %shard_map.69 = (f32[4,8,8,128]{3,2,1,0:T(8,128)}, bf16[4,8,8,128]{3,2,1,0:T(8,128)(2,1)}) custom-call(f32[4,8,8,128]{3,2,1,0:T(8,128)S(1)} %get-tuple-element.4.sol_in, f32[4,8,8,128]{3,2,1,0:T(8,128)S(1)} %get-tuple-element.5.new_in), custom_call_target="tpu_custom_call" | custom-call | tf_op jit(solution)/shard_map/pallas_call | solution.py:428

commit v4 on v3

--- a/solution.py
+++ b/solution.py
@@ -46,6 +46,11 @@
     inside = inside + jnp.where(row == col, ends, 0.0)
     inside = inside - jnp.where((col == row + 1) & last, penalty, 0.0)
     return inside - jnp.where((col == row - 1) & first, penalty, 0.0)
+
+
+def halves(values):
+    high = values.astype(jnp.bfloat16)
+    return high, (values - high.astype(jnp.float32)).astype(jnp.bfloat16)
 
 
 def kernel(
@@ -64,6 +69,8 @@
     moves = offsets(sizes)
     unrolled = len(moves) <= 64
     inverse = 1.0 / total_points
+    at_q, at_m = solves * keep, 2 * solves * keep
+    at_rest = at_m + 4 * solves
 
     def partner(move):
         return {
@@ -209,13 +216,15 @@
     )
 
     row, col = iota((size_z, size_z), 0), iota((size_z, size_z), 1)
-    mat_z[...] = line_matrix(stiffness[...], row, col)
+    full_z = line_matrix(stiffness[...], row, col)
     area = size_x * size_y
     row, col = iota((area, area), 0), iota((area, area), 1)
     row_x, col_x, row_y, col_y = row // size_y, col // size_y, row % size_y, col % size_y
-    mat_xy[...] = jnp.where(
+    full_xy = jnp.where(
         row_y == col_y, line_matrix(stiffness[...], row_x, col_x), 0.0
     ) + jnp.where(row_x == col_x, line_matrix(stiffness[...], row_y, col_y), 0.0)
+    for kept, full in ((mat_z, full_z), (mat_xy, full_xy)):
+        kept[0], kept[1] = halves(full)
     pairs = [(k, l) for k in range(keep) for l in range(k, keep)]
     gram = [inner(wide[s, k], wide[s, l]) for s in range(solves) for k, l in pairs]
     rows2[1:2] = row_of(gram[:LANES])
@@ -239,8 +248,10 @@
 
     def local(field, s):
         flat = field[s].reshape(area, size_z)
-        along_z = jnp.dot(flat, mat_z[...], precision=highest, preferred_element_type=jnp.float32)
-        along_xy = jnp.dot(mat_xy[...], flat, precision=highest, preferred_element_type=jnp.float32)
+        high, low = halves(flat)
+        dot = functools.partial(jnp.dot, preferred_element_type=jnp.float32)
+        along_z = dot(high, mat_z[0]) + (dot(low, mat_z[0]) + dot(high, mat_z[1]))
+        along_xy = dot(mat_xy[0], high) + (dot(mat_xy[1], high) + dot(mat_xy[0], low))
         out = (along_z + along_xy).reshape(size_x, size_y, size_z)
         return out + helm[s] * inertia[...] * field[s]
 
@@ -321,17 +332,17 @@
         moments.append(
             [inner(r0[s], r0[s]), inner(r0[s], q[s]), inner(q[s], q[s]), inner(q[s], local(q, s))]
         )
+    flat_moments = [moments[s][j] for s in range(solves) for j in range(4)]
+    most = row_of(with_r + with_q + flat_moments + gram_rest)
     finish()
-    for s in range(solves):
-        moments[s][3] = moments[s][3] - inner(q[s], received(1, s))
-    flat_moments = [moments[s][j] for s in range(solves) for j in range(4)]
-    rows2[0:1] = row_of(with_r + with_q + flat_moments + gram_rest)
+    late = [jnp.zeros((size_y, size_z), jnp.float32)] * (at_m + 4 * solves)
+    for s in range(solves):
+        late[at_m + 4 * s + 3] = inner(q[s], received(1, s))
+    rows2[0:1] = most - row_of(late)
     send_all(rows2, got2, send2, recv2)
     take_all(got2, send2, recv2)
     sums = (rows2[...] + jnp.sum(got2[...], axis=0)) * inverse
     main, other = sums[0:1], sums[1:2]
-    at_q, at_m = solves * keep, 2 * solves * keep
-    at_rest = at_m + 4 * solves
 
     for s in range(solves):
         coef = [splat(coefs, s * keep + k) for k in range(keep)]
@@ -400,8 +411,8 @@
             pltpu.SemaphoreType.DMA((4,)),
             pltpu.VMEM(basis.shape, jnp.float32),
             field, field, field,
-            pltpu.VMEM((size_z, size_z), jnp.float32),
-            pltpu.VMEM((area, area), jnp.float32),
+            pltpu.VMEM((2, size_z, size_z), jnp.bfloat16),
+            pltpu.VMEM((2, area, area), jnp.bfloat16),
             pltpu.VMEM((*faces, size_x, size_z), jnp.float32),
             pltpu.VMEM((EXCHANGES, 2, size_y, size_z), jnp.float32),
             pltpu.VMEM((*faces, size_y, size_z), jnp.float32),

time: 26.5 us -> 26.3 us (level)
  no operation moved by 1% of the time
where the time goes in v4:
time: 26.3 us; the launch traced here: 26.1 us
  Pallas kernels  25.5 us (97%)
  between operations  0.64 us (2%)
    pallas_call x1, Pallas kernels, on_device(): pl.pallas_call(functools.partial(kernel, sizes, total_points), out_shape=...  24.8 us
    pallas_call x1, Pallas kernels, on_device(): pl.pallas_call(write, out_shape=(jax.ShapeDtypeStruct(rhs.shape, jnp.floa...  0.69 us

profile of v4, /device:TPU:0, one launch (start us, length us, event | category | flops | bytes accessed | tf_op | source)
XLA Modules:
  0.0 26.1 jit_solution(5397242597302118798)
XLA Ops:
  0.6 24.8 %shard_map.68 = (f32[4,8,8,128]{3,2,1,0:T(8,128)S(1)}, f32[4,8,8,128]{3,2,1,0:T(8,128)S(1)}) custom-call(f32[4,8,8,128]{3,2,1,0:T(8,128)} %rhs_any.1, bf16[4,8,8,8,128]{4,3,2,1,0:T(8,128)(2,1)} %basis_any.1, f32[8,8,128]{2,1,0:T(8,128)} %inertia_any.1, f32[4]{0:T(128)} %helm.1, f32[8,8]{1,0:T(8,128)} %stiffness_any.1), custom_call_target="tpu_custom_call" | custom-call | tf_op jit(solution)/shard_map/pallas_call | solution.py:401
  25.4 0.7 %shard_map.69 = (f32[4,8,8,128]{3,2,1,0:T(8,128)}, bf16[4,8,8,128]{3,2,1,0:T(8,128)(2,1)}) custom-call(f32[4,8,8,128]{3,2,1,0:T(8,128)S(1)} %get-tuple-element.4.sol_in, f32[4,8,8,128]{3,2,1,0:T(8,128)S(1)} %get-tuple-element.5.new_in), custom_call_target="tpu_custom_call" | custom-call | tf_op jit(solution)/shard_map/pallas_call | solution.py:439
